TPU v7x, 32 devices: a whole 2x2x4 slice. The times are simulated.
32 devices in a mesh: ulysses: 8 (over z, x), blk: 4 (over y, core).
Axes of the slice: x: 2, y: 2, z: 4, core: 2. Of those that a mesh axis runs over, the one named last changes fastest.
Arguments:
- queries: bfloat16 [4, 512, 4096], P('blk', 'ulysses'), may hold values from -6 to 6
- key_rows: bfloat16 [4, 512, 1024], P('blk', 'ulysses'), may hold values from -6 to 6
- value_rows: bfloat16 [4, 512, 1024], P('blk', 'ulysses'), may hold values from -6 to 6
- tile_segment: int32 [16], replicated, may hold values from 0 to 3, never falling along the last dimension, each value on 1 to 8 neighbouring positions
Outputs:
- attended: bfloat16 [4, 512, 4096], P('blk', 'ulysses')
Inputs may be any that keep to these rules, and one draw needn't show every extreme that they name: `tile_segment`: segment numbers never fall along the sequence and each segment covers 1 to 8 tiles.
All inputs are finite; a program needn't handle non-finite values.
Results may differ from a plain program's by a relative error of at most 0.0045.
Values may be sent and summed in bfloat16 or wider, within the bound.
A program may use at most 64 MiB of HBM per device.

v0:
```python
import math
import jax
import jax.numpy as jnp
from jax import lax
from jax.sharding import PartitionSpec as P

HEAD_DIM = 128
TILE = 128
masked_score = -1e30


def segment_of(positions, tile_segment):
    tiles_total = tile_segment.shape[0]
    matches = (positions // TILE)[:, None] == jnp.arange(tiles_total, dtype=jnp.int32)[None, :]
    return jnp.sum(jnp.where(matches, tile_segment[None, :], 0), axis=1)


def visible(query_pos, query_seg, key_pos, key_seg):
    earlier = key_pos[None, :] <= query_pos[:, None]
    same_image = (key_seg[None, :] == query_seg[:, None]) & (query_seg[:, None] % 2 == 1)
    return earlier | same_image


def widen(source_rows, groups):
    tokens_dev = source_rows.shape[1]
    heads_here = source_rows.shape[2] // HEAD_DIM
    factor = max(1, groups // heads_here)
    spread = jnp.repeat(source_rows.reshape(1, tokens_dev, heads_here, HEAD_DIM), factor, axis=2)
    return spread.reshape(1, tokens_dev, heads_here * factor * HEAD_DIM)


def same_rows(row_ids):
    return row_ids


def update(current, allowed, query_block, key_block, value_block):
    maxima, denominators, weighted = current
    scores = jnp.einsum(
        "qkgd,skd->kgqs", query_block, key_block, preferred_element_type=jnp.float32
    )
    scores = jnp.where(allowed[None, None], scores * HEAD_DIM ** (-0.5), masked_score)
    new_max = jnp.maximum(maxima, jnp.max(scores, axis=3))
    weights = jnp.where(allowed[None, None], jnp.exp(scores - new_max[..., None]), 0.0)
    factor = jnp.exp(maxima - new_max)
    denominators = factor * denominators + jnp.sum(weights, axis=3)
    product = jnp.einsum(
        "kgqs,skd->kgqd",
        weights.astype(jnp.bfloat16),
        value_block,
        preferred_element_type=jnp.float32,
    )
    weighted = factor[..., None] * weighted + product
    return (new_max, denominators, weighted)


def keep_state(current, allowed, query_block, key_block, value_block):
    return current


def build_fold(query_rows, query_pos, tile_segment, key_position, kv_width):
    rows_total = query_rows.shape[0]
    kv_local = kv_width // HEAD_DIM
    group_size = query_rows.shape[1] // HEAD_DIM // kv_local
    shaped = query_rows.reshape(rows_total, kv_local, group_size, HEAD_DIM)
    query_seg = segment_of(query_pos, tile_segment)
    half_rows = rows_total // 2

    def fold_step(running, portion, offset):
        key_part, value_part = portion
        portion_rows = key_part.shape[0]
        block_rows = math.gcd(portion_rows, 512)
        block_total = portion_rows // block_rows
        key_blocks = key_part.reshape(block_total, block_rows, kv_local, HEAD_DIM)
        value_blocks = value_part.reshape(block_total, block_rows, kv_local, HEAD_DIM)

        def one_block(halves, inputs):
            key_block, value_block, block_number = inputs
            key_pos = key_position(
                block_number * block_rows + jnp.arange(block_rows, dtype=jnp.int32)
            )
            key_seg = segment_of(key_pos, tile_segment)
            results = []
            for half_index in range(2):
                row_low = half_index * half_rows
                row_high = row_low + half_rows
                allowed = visible(
                    query_pos[row_low:row_high], query_seg[row_low:row_high], key_pos, key_seg
                )
                results.append(
                    lax.cond(
                        jnp.any(allowed),
                        update,
                        keep_state,
                        halves[half_index],
                        allowed,
                        shaped[row_low:row_high],
                        key_block,
                        value_block,
                    )
                )
            return ((results[0], results[1]), None)

        running, unused = lax.scan(
            one_block, running, (key_blocks, value_blocks, jnp.arange(block_total, dtype=jnp.int32))
        )
        return running

    def empty_half():
        return (
            jnp.full((kv_local, group_size, half_rows), masked_score, jnp.float32),
            jnp.zeros((kv_local, group_size, half_rows), jnp.float32),
            jnp.zeros((kv_local, group_size, half_rows, HEAD_DIM), jnp.float32),
        )

    return (fold_step, (empty_half(), empty_half()))


def finish(running):
    outputs = [weighted / denominators[..., None] for maxima, denominators, weighted in running]
    joined = jnp.concatenate(outputs, axis=2)
    kv_local, group_size, rows_total, head_dim = joined.shape
    joined = jnp.transpose(joined, (2, 0, 1, 3)).reshape(
        rows_total, kv_local * group_size * head_dim
    )
    return joined.astype(jnp.bfloat16)


def local(queries, key_rows, value_rows, tile_segment):
    ulysses_count = lax.axis_size("ulysses")
    tokens_dev = queries.shape[1]
    block_len = tokens_dev * ulysses_count
    block_index = lax.axis_index("blk")
    local_rows = jnp.arange(block_len, dtype=jnp.int32)
    moved = (
        lax.all_to_all(queries, "ulysses", split_axis=2, concat_axis=1, tiled=True),
        lax.all_to_all(
            widen(key_rows, ulysses_count), "ulysses", split_axis=2, concat_axis=1, tiled=True
        ),
        lax.all_to_all(
            widen(value_rows, ulysses_count), "ulysses", split_axis=2, concat_axis=1, tiled=True
        ),
    )
    query_rows, key_local, value_local = (moved[0][0], moved[1][0], moved[2][0])
    query_pos = block_index * block_len + local_rows
    fold_step, initial = build_fold(
        query_rows, query_pos, tile_segment, same_rows, key_local.shape[1]
    )
    running = fold_step(
        initial,
        (
            lax.all_gather(key_local, "blk", axis=0, tiled=True),
            lax.all_gather(value_local, "blk", axis=0, tiled=True),
        ),
        jnp.int32(0),
    )
    attended = lax.all_to_all(
        finish(running)[None], "ulysses", split_axis=1, concat_axis=2, tiled=True
    )
    return attended


def solution(mesh):
    return jax.shard_map(
        local,
        mesh=mesh,
        in_specs=(
            P("blk", "ulysses", None),
            P("blk", "ulysses", None),
            P("blk", "ulysses", None),
            P(),
        ),
        out_specs=P("blk", "ulysses", None),
        check_vma=False,
    )
```

profile of v0, /device:TPU:4, one launch (start us, length us, event | category | flops | bytes accessed | tf_op | source)
XLA Modules:
  0.0 138.4 jit_solution(7677934682182908862)
XLA Ops:
  0.0 1.3 copy.59
  1.3 0.6 broadcast.215
  1.9 2.3 %reduce.4 = bf16[1024,64]{1,0:T(8,128)(2,1)S(1)} reduce(bf16[1024,1,64]{2,1,0:T(2,128)(2,1)S(1)} %bitcast.162, bf16[]{:T(256)} %broadcast.215), dimensions={1}, to_apply=%bitcast.126.reduce_sub_computation | reduce | bytes 262146
  4.2 0.9 reshape.154
  5.1 5.8 %all-to-all-start = ((bf16[8,2,4096]{2,1,0:T(2,128)(2,1)}), bf16[8,2,4096]{2,1,0:T(2,128)(2,1)S(1)}, u32[]{:S(2)}, u32[]{:S(2)}) async-start(bf16[8,2,4096]{2,1,0:T(2,128)(2,1)} %reshape.154), calls=%async_computation | async-start | bytes 262144 | tf_op jit(solution)/shard_map/all_to_all | solution.py:136
  11.3 2.3 %reduce.5 = bf16[1024,64]{1,0:T(8,128)(2,1)S(1)} reduce(bf16[1024,1,64]{2,1,0:T(2,128)(2,1)S(1)} %bitcast.163, bf16[]{:T(256)} %broadcast.215), dimensions={1}, to_apply=%bitcast.128.reduce_sub_computation | reduce | bytes 262146
  13.6 0.9 reshape.156
  14.5 3.7 %all-to-all-done = bf16[8,2,4096]{2,1,0:T(2,128)(2,1)S(1)} async-done(((bf16[8,2,4096]{2,1,0:T(2,128)(2,1)}), bf16[8,2,4096]{2,1,0:T(2,128)(2,1)S(1)}, u32[]{:S(2)}, u32[]{:S(2)}) %all-to-all-start) | async-done | bytes 131104 | tf_op jit(solution)/shard_map/all_to_all | solution.py:136
  18.2 3.4 %all-to-all-start.1 = ((bf16[8,2,4096]{2,1,0:T(2,128)(2,1)}), bf16[8,2,4096]{2,1,0:T(2,128)(2,1)S(1)}, u32[]{:S(2)}, u32[]{:S(2)}) async-start(bf16[8,2,4096]{2,1,0:T(2,128)(2,1)} %reshape.156), calls=%async_computation.1 | async-start | bytes 262144 | tf_op jit(solution)/shard_map/all_to_all | solution.py:139
  21.6 2.8 %copy.65 = bf16[1,64,4096]{1,0,2:T(2,128)(2,1)S(1)} copy(bf16[1,64,4096]{2,1,0:T(8,128)(2,1)S(1)} %copy-done) | data formatting | bytes 1048576 | tf_op args[0]
  24.4 22.5 %reduce.6 = bf16[4096,64]{1,0:T(8,128)(2,1)S(1)} reduce(bf16[4096,1,64]{2,1,0:T(2,128)(2,1)S(1)} %bitcast.152, bf16[]{:T(256)} %broadcast.215), dimensions={1}, to_apply=%bitcast.130.reduce_sub_computation | reduce | bytes 1048578
  46.9 1.5 %reshape.158 = bf16[8,2,16384]{2,1,0:T(2,128)(2,1)} reshape(bf16[4096,64]{1,0:T(8,128)(2,1)S(1)} %reduce.6) | data formatting | bytes 1048576
  48.5 5.9 %all-to-all-start.2 = ((bf16[8,2,16384]{2,1,0:T(2,128)(2,1)}), bf16[8,2,16384]{2,1,0:T(2,128)(2,1)}, u32[]{:S(2)}, u32[]{:S(2)}) async-start(bf16[8,2,16384]{2,1,0:T(2,128)(2,1)} %reshape.158), calls=%async_computation.2 | async-start | bytes 1048576 | tf_op jit(solution)/shard_map/all_to_all | solution.py:135
  55.9 6.7 %all_gather.6 = bf16[2048,128]{1,0:T(8,128)(2,1)S(1)} all-gather(bf16[512,128]{1,0:T(8,128)(2,1)S(1)} %bitcast.169), channel_id=1, replica_groups=mesh['ulysses'=8,'blk'=4] {'blk'}, dimensions={0}, use_global_device_ids=true | all-gather | bytes 655360 | tf_op jit(solution)/shard_map/all_gather | solution.py:151
  62.6 7.3 %all_gather.7 = bf16[2048,128]{1,0:T(8,128)(2,1)S(1)} all-gather(bf16[512,128]{1,0:T(8,128)(2,1)S(1)} %bitcast.170), channel_id=1, replica_groups=mesh['ulysses'=8,'blk'=4] {'blk'}, dimensions={0}, use_global_device_ids=true | all-gather | bytes 655360 | tf_op jit(solution)/shard_map/all_gather | solution.py:152
  69.9 4.1 %reshape.159 = bf16[4096,1,64]{2,1,0:T(2,128)(2,1)S(1)} reshape(bf16[8,2,16384]{2,1,0:T(2,128)(2,1)} %all-to-all-done.2) | data formatting | bytes 1048576
  74.0 3.6 %copy.66 = bf16[1,64,4096]{2,1,0:T(8,128)(2,1)} copy(bf16[1,64,4096]{1,0,2:T(2,128)(2,1)S(1)} %bitcast.151) | data formatting | bytes 1048576 | tf_op jit(solution)/shard_map/all_to_all | solution.py:135
  77.6 1.2 copy.81
  79.4 31.0 %while.23 = (s32[]{:T(128)}, f32[1,4,256]{2,1,0:T(4,128)S(1)}, f32[1,4,256]{2,1,0:T(4,128)S(1)}, f32[1,4,256,128]{3,2,1,0:T(8,128)S(1)}, f32[1,4,256]{2,1,0:T(4,...) while((s32[]{:T(128)}, f32[1,4,256]{2,1,0:T(4,128)S(1)}, ...), condition=%wide.region_13.14_spmd, body=%wide.region_1.13_spmd.sunk | while | flops 552381440 | bytes 17462768 | solution.py:103
  79.4 0.6 dynamic_slice.28
  80.8 1.1 fusion.59
  82.5 1.9 %conditional.5 = ((f32[1,4,256]{2,1,0:T(4,128)S(1)}, f32[1,4,256]{2,1,0:T(4,128)S(1)}, f32[1,4,256,128]{3,2,1,0:T(8,128)S(1)})) conditional(s32[]{:T(128)} %convert_element_type.47, (f32[1,4,256]{2,1,0:T(4,128)S(1)}, f32[1,4,256]{2,1,0:T(4,128)S(1)}, f32[1,4,256,128]{3,2,1,0:T(8,128)S(1)}) %tuple.82, (pred[256,512]{0,1:T(8,128)(4,1)S(1)}, ...), branch_computations={%region_9.9_spmd, %region_10.12_spmd} | conditional | flops 275516416 | bytes 8323104 | solution.py:90
  82.5 0.5 fusion.20
  83.0 0.5 fusion.22
  83.6 0.9 fusion.23
  85.2 2.0 %conditional.4 = ((f32[1,4,256]{2,1,0:T(4,128)S(1)}, f32[1,4,256]{2,1,0:T(4,128)S(1)}, f32[1,4,256,128]{3,2,1,0:T(8,128)S(1)})) conditional(s32[]{:T(128)} %convert_element_type.46, (f32[1,4,256]{2,1,0:T(4,128)S(1)}, f32[1,4,256]{2,1,0:T(4,128)S(1)}, f32[1,4,256,128]{3,2,1,0:T(8,128)S(1)}) %tuple.80, (pred[256,512]{0,1:T(8,128)(4,1)S(1)}, ...), branch_computations={%region_4.4_spmd, %region_5.7_spmd} | conditional | flops 275516416 | bytes 8323104 | solution.py:90
  85.2 0.5 fusion
  85.7 0.5 fusion.2
  86.2 0.9 fusion.3
  87.1 0.6 dynamic_slice.28
  88.5 1.1 fusion.59
  90.3 2.0 %conditional.5 = ((f32[1,4,256]{2,1,0:T(4,128)S(1)}, f32[1,4,256]{2,1,0:T(4,128)S(1)}, f32[1,4,256,128]{3,2,1,0:T(8,128)S(1)})) conditional(s32[]{:T(128)} %convert_element_type.47, (f32[1,4,256]{2,1,0:T(4,128)S(1)}, f32[1,4,256]{2,1,0:T(4,128)S(1)}, f32[1,4,256,128]{3,2,1,0:T(8,128)S(1)}) %tuple.82, (pred[256,512]{0,1:T(8,128)(4,1)S(1)}, ...), branch_computations={%region_9.9_spmd, %region_10.12_spmd} | conditional | flops 275516416 | bytes 8323104 | solution.py:90
  90.3 0.5 fusion.20
  90.8 0.5 fusion.22
  91.3 0.9 fusion.23
  92.9 2.0 %conditional.4 = ((f32[1,4,256]{2,1,0:T(4,128)S(1)}, f32[1,4,256]{2,1,0:T(4,128)S(1)}, f32[1,4,256,128]{3,2,1,0:T(8,128)S(1)})) conditional(s32[]{:T(128)} %convert_element_type.46, (f32[1,4,256]{2,1,0:T(4,128)S(1)}, f32[1,4,256]{2,1,0:T(4,128)S(1)}, f32[1,4,256,128]{3,2,1,0:T(8,128)S(1)}) %tuple.80, (pred[256,512]{0,1:T(8,128)(4,1)S(1)}, ...), branch_computations={%region_4.4_spmd, %region_5.7_spmd} | conditional | flops 275516416 | bytes 8323104 | solution.py:90
  92.9 0.5 fusion
  93.4 0.5 fusion.2
  94.0 0.9 fusion.3
  94.9 0.6 dynamic_slice.28
  96.3 1.1 fusion.59
  98.0 1.9 %conditional.5 = ((f32[1,4,256]{2,1,0:T(4,128)S(1)}, f32[1,4,256]{2,1,0:T(4,128)S(1)}, f32[1,4,256,128]{3,2,1,0:T(8,128)S(1)})) conditional(s32[]{:T(128)} %convert_element_type.47, (f32[1,4,256]{2,1,0:T(4,128)S(1)}, f32[1,4,256]{2,1,0:T(4,128)S(1)}, f32[1,4,256,128]{3,2,1,0:T(8,128)S(1)}) %tuple.82, (pred[256,512]{0,1:T(8,128)(4,1)S(1)}, ...), branch_computations={%region_9.9_spmd, %region_10.12_spmd} | conditional | flops 275516416 | bytes 8323104 | solution.py:90
  98.0 0.5 fusion.20
  98.5 0.5 fusion.22
  99.1 0.9 fusion.23
  100.7 2.0 %conditional.4 = ((f32[1,4,256]{2,1,0:T(4,128)S(1)}, f32[1,4,256]{2,1,0:T(4,128)S(1)}, f32[1,4,256,128]{3,2,1,0:T(8,128)S(1)})) conditional(s32[]{:T(128)} %convert_element_type.46, (f32[1,4,256]{2,1,0:T(4,128)S(1)}, f32[1,4,256]{2,1,0:T(4,128)S(1)}, f32[1,4,256,128]{3,2,1,0:T(8,128)S(1)}) %tuple.80, (pred[256,512]{0,1:T(8,128)(4,1)S(1)}, ...), branch_computations={%region_4.4_spmd, %region_5.7_spmd} | conditional | flops 275516416 | bytes 8323104 | solution.py:90
  100.7 0.5 fusion
  101.2 0.5 fusion.2
  101.7 0.9 fusion.3
  102.7 0.6 dynamic_slice.28
  104.0 1.1 fusion.59
  105.8 2.0 %conditional.5 = ((f32[1,4,256]{2,1,0:T(4,128)S(1)}, f32[1,4,256]{2,1,0:T(4,128)S(1)}, f32[1,4,256,128]{3,2,1,0:T(8,128)S(1)})) conditional(s32[]{:T(128)} %convert_element_type.47, (f32[1,4,256]{2,1,0:T(4,128)S(1)}, f32[1,4,256]{2,1,0:T(4,128)S(1)}, f32[1,4,256,128]{3,2,1,0:T(8,128)S(1)}) %tuple.82, (pred[256,512]{0,1:T(8,128)(4,1)S(1)}, ...), branch_computations={%region_9.9_spmd, %region_10.12_spmd} | conditional | flops 275516416 | bytes 8323104 | solution.py:90
  105.8 0.5 fusion.20
  106.3 0.5 fusion.22
  106.9 0.9 fusion.23
  108.4 2.0 %conditional.4 = ((f32[1,4,256]{2,1,0:T(4,128)S(1)}, f32[1,4,256]{2,1,0:T(4,128)S(1)}, f32[1,4,256,128]{3,2,1,0:T(8,128)S(1)})) conditional(s32[]{:T(128)} %convert_element_type.46, (f32[1,4,256]{2,1,0:T(4,128)S(1)}, f32[1,4,256]{2,1,0:T(4,128)S(1)}, f32[1,4,256,128]{3,2,1,0:T(8,128)S(1)}) %tuple.80, (pred[256,512]{0,1:T(8,128)(4,1)S(1)}, ...), branch_computations={%region_4.4_spmd, %region_5.7_spmd} | conditional | flops 275516416 | bytes 8323104 | solution.py:90
  108.4 0.5 fusion
  109.0 0.5 fusion.2
  109.5 0.9 fusion.3
  111.0 0.9 copy.73
  111.9 3.9 %reduce.7 = bf16[512,512]{1,0:T(8,128)(2,1)S(1)} reduce(bf16[512,1,512]{2,1,0:T(2,128)(2,1)S(1)} %bitcast.154, bf16[]{:T(256)} %broadcast.215), dimensions={1}, to_apply=%bitcast.132.reduce_sub_computation | reduce | bytes 1048578
  116.1 20.8 %all_to_all.63 = bf16[8,2,16384]{2,1,0:T(2,128)(2,1)S(1)} all-to-all(bf16[8,2,16384]{2,1,0:T(2,128)(2,1)S(1)} %reshape.160), channel_id=1, replica_groups=mesh['ulysses'=8,'blk'=4] {'ulysses'}, dimensions={0} | all-to-all | bytes 1048576 | tf_op jit(solution)/shard_map/all_to_all | solution.py:156
  136.9 0.5 reshape.161
  137.6 0.8 copy.78
  (84 shorter events, 4.2 us)
Async XLA Ops:
  0.0 10.9 %copy-start.1 = (bf16[1,64,1024]{2,1,0:T(8,128)(2,1)S(1)}, bf16[1,64,1024]{2,1,0:T(8,128)(2,1)}, u32[]{:S(2)}) copy-start(bf16[1,64,1024]{2,1,0:T(8,128)(2,1)} %param.12) | copy-start | bytes 393220
  0.0 21.6 %copy-start = (bf16[1,64,4096]{2,1,0:T(8,128)(2,1)S(1)}, bf16[1,64,4096]{2,1,0:T(8,128)(2,1)}, u32[]{:S(2)}) copy-start(bf16[1,64,4096]{2,1,0:T(8,128)(2,1)} %param.10) | copy-start | bytes 1572868
  5.1 13.1 %all-to-all-start = ((bf16[8,2,4096]{2,1,0:T(2,128)(2,1)}), bf16[8,2,4096]{2,1,0:T(2,128)(2,1)S(1)}, u32[]{:S(2)}, u32[]{:S(2)}) async-start(bf16[8,2,4096]{2,1,0:T(2,128)(2,1)} %reshape.154), calls=%async_computation | async-start | bytes 262144 | tf_op jit(solution)/shard_map/all_to_all | solution.py:136
  18.2 30.3 %all-to-all-start.1 = ((bf16[8,2,4096]{2,1,0:T(2,128)(2,1)}), bf16[8,2,4096]{2,1,0:T(2,128)(2,1)S(1)}, u32[]{:S(2)}, u32[]{:S(2)}) async-start(bf16[8,2,4096]{2,1,0:T(2,128)(2,1)} %reshape.156), calls=%async_computation.1 | async-start | bytes 262144 | tf_op jit(solution)/shard_map/all_to_all | solution.py:139
  24.4 24.0 %copy-start.2 = (s32[16]{0:T(128)S(1)}, s32[16]{0:T(128)}, u32[]{:S(2)}) copy-start(s32[16]{0:T(128)} %param.13) | copy-start | bytes 196
  48.5 21.3 %all-to-all-start.2 = ((bf16[8,2,16384]{2,1,0:T(2,128)(2,1)}), bf16[8,2,16384]{2,1,0:T(2,128)(2,1)}, u32[]{:S(2)}, u32[]{:S(2)}) async-start(bf16[8,2,16384]{2,1,0:T(2,128)(2,1)} %reshape.158), calls=%async_computation.2 | async-start | bytes 1048576 | tf_op jit(solution)/shard_map/all_to_all | solution.py:135
where the time goes:
time: 139 us; the launch traced here: 138 us
  other arithmetic  40.5 us (29%)
  blocking collectives  34.7 us (25%)
  local copies, waits for them, and re-layouts  24.7 us (18%)
  starting transfers between devices  15.1 us (11%)
  matrix products  10.8 us (8%)
  loops' own time  8.49 us (6%)
  waiting for transfers between devices  3.74 us (3%)
    unnamed x4, other arithmetic  31 us
    all_to_all x1, blocking collectives, local(): lax.all_to_all(finish(running)[None], 'ulysses', split_axis=1, concat_axi...  20.8 us
    unnamed x22, local copies, waits for them, and re-layouts  15.4 us
    another operation x1, loops' own time, fold_step(): lax.scan(one_block, running, (key_blocks, value_blocks, jnp.arange(block_...  8.16 us
    all_gather x1, blocking collectives, local(): lax.all_gather(value_local, 'blk', axis=0, tiled=True)  7.26 us
    dot_general x8, matrix products, update(): jnp.einsum('kgqs,skd->kgqd', weights.astype(jnp.bfloat16), value_block, p...  6.93 us
    all_gather x1, blocking collectives, local(): lax.all_gather(key_local, 'blk', axis=0, tiled=True)  6.68 us
    all_to_all x1, starting transfers between devices, local(): lax.all_to_all(queries, 'ulysses', split_axis=2, concat_axis=1, tiled=True)  5.9 us
  transfers between devices with their start and end apart: 3, of which 1 were waited for; matrix products, arithmetic and copies ran while one was open for 23% of the time, Pallas kernels for 0%

commit v1 on v0

--- a/solution.py
+++ b/solution.py
@@ -7,6 +7,12 @@
 HEAD_DIM = 128
 TILE = 128
 masked_score = -1e30
+
+
+def gather_by_exchange(x, axis, dim):
+    size = lax.axis_size(axis)
+    repeats = [size if d == dim else 1 for d in range(x.ndim)]
+    return lax.all_to_all(jnp.tile(x, repeats), axis, split_axis=dim, concat_axis=dim, tiled=True)
 
 
 def segment_of(positions, tile_segment):
@@ -149,7 +155,7 @@
         initial,
         (
             lax.all_gather(key_local, "blk", axis=0, tiled=True),
-            lax.all_gather(value_local, "blk", axis=0, tiled=True),
+            gather_by_exchange(value_local, "blk", 0),
         ),
         jnp.int32(0),
     )

time: 139 us -> 150 us (1.079)
  waiting for transfers between devices: 3.74 us -> 14.9 us
  blocking collectives: 34.7 us -> 29.3 us
  starting transfers between devices: 15.1 us -> 19 us
    all_to_all x1, waiting for transfers between devices: 0.01 us -> 11.2 us  [local(): lax.all_to_all(queries, 'ulysses', split_axis=2, concat_axis=1, tiled=True)]
    all_gather x1 -> x0, blocking collectives: 7.26 us -> none  [local(): lax.all_gather(value_local, 'blk', axis=0, tiled=True)]
    all_gather x1, blocking collectives: 6.68 us -> 10.9 us  [local(): lax.all_gather(key_local, 'blk', axis=0, tiled=True)]
    all_to_all x0 -> x1, starting transfers between devices: none -> 3.95 us  [gather_by_exchange(): lax.all_to_all(jnp.tile(x, repeats), axis, split_axis=dim, concat_axis=di...]
    all_to_all x1, waiting for transfers between devices: 3.74 us -> 0.01 us  [local(): lax.all_to_all(widen(key_rows, ulysses_count), 'ulysses', split_axis=2, c...]
    all_to_all x1, waiting for transfers between devices: 0.01 us -> 3.74 us  [local(): lax.all_to_all(widen(value_rows, ulysses_count), 'ulysses', split_axis=2,...]
    all_to_all x1, starting transfers between devices: 5.81 us -> 3.37 us  [local(): lax.all_to_all(widen(key_rows, ulysses_count), 'ulysses', split_axis=2, c...]
    all_to_all x1, starting transfers between devices: 3.37 us -> 5.81 us  [local(): lax.all_to_all(widen(value_rows, ulysses_count), 'ulysses', split_axis=2,...]
  transfers between devices with their start and end apart: 3 -> 4, of which waited for: 1 -> 2; matrix products, arithmetic and copies ran while one was open for 23% -> 28% of each run, Pallas kernels for 0% -> 0%
where the time goes in v1:
time: 150 us; the launch traced here: 149 us
  other arithmetic  40.5 us (27%)
  blocking collectives  29.3 us (20%)
  local copies, waits for them, and re-layouts  25.7 us (17%)
  starting transfers between devices  19 us (13%)
  waiting for transfers between devices  14.9 us (10%)
  matrix products  10.8 us (7%)
  loops' own time  8.49 us (6%)
    unnamed x4, other arithmetic  31 us
    all_to_all x1, blocking collectives, local(): lax.all_to_all(finish(running)[None], 'ulysses', split_axis=1, concat_axi...  18.5 us
    unnamed x24, local copies, waits for them, and re-layouts  15.4 us
    all_to_all x1, waiting for transfers between devices, local(): lax.all_to_all(queries, 'ulysses', split_axis=2, concat_axis=1, tiled=True)  11.2 us
    all_gather x1, blocking collectives, local(): lax.all_gather(key_local, 'blk', axis=0, tiled=True)  10.9 us
    another operation x1, loops' own time, fold_step(): lax.scan(one_block, running, (key_blocks, value_blocks, jnp.arange(block_...  8.16 us
    dot_general x8, matrix products, update(): jnp.einsum('kgqs,skd->kgqd', weights.astype(jnp.bfloat16), value_block, p...  6.93 us
    all_to_all x1, starting transfers between devices, local(): lax.all_to_all(queries, 'ulysses', split_axis=2, concat_axis=1, tiled=True)  5.9 us
  transfers between devices with their start and end apart: 4, of which 2 were waited for; matrix products, arithmetic and copies ran while one was open for 28% of the time, Pallas kernels for 0%

profile of v1, /device:TPU:4, one launch (start us, length us, event | category | flops | bytes accessed | tf_op | source)
XLA Modules:
  0.0 149.1 jit_solution(11274781889114034909)
XLA Ops:
  0.0 1.3 copy.61
  1.3 0.6 broadcast.217
  1.9 2.3 %reduce.5 = bf16[1024,64]{1,0:T(8,128)(2,1)S(1)} reduce(bf16[1024,1,64]{2,1,0:T(2,128)(2,1)S(1)} %bitcast.160, bf16[]{:T(256)} %broadcast.217), dimensions={1}, to_apply=%bitcast.126.reduce_sub_computation | reduce | bytes 262146
  4.2 0.9 reshape.164
  5.1 5.8 %all-to-all-start.1 = ((bf16[8,2,4096]{2,1,0:T(2,128)(2,1)}), bf16[8,2,4096]{2,1,0:T(2,128)(2,1)S(1)}, u32[]{:S(2)}, u32[]{:S(2)}) async-start(bf16[8,2,4096]{2,1,0:T(2,128)(2,1)} %reshape.164), calls=%async_computation.1 | async-start | bytes 262144 | tf_op jit(solution)/shard_map/all_to_all | solution.py:145
  11.3 2.3 %reduce.4 = bf16[1024,64]{1,0:T(8,128)(2,1)S(1)} reduce(bf16[1024,1,64]{2,1,0:T(2,128)(2,1)S(1)} %bitcast.161, bf16[]{:T(256)} %broadcast.217), dimensions={1}, to_apply=%bitcast.124.reduce_sub_computation | reduce | bytes 262146
  13.6 0.9 reshape.162
  14.5 3.7 %all-to-all-done.1 = bf16[8,2,4096]{2,1,0:T(2,128)(2,1)S(1)} async-done(((bf16[8,2,4096]{2,1,0:T(2,128)(2,1)}), bf16[8,2,4096]{2,1,0:T(2,128)(2,1)S(1)}, u32[]{:S(2)}, u32[]{:S(2)}) %all-to-all-start.1) | async-done | bytes 131104 | tf_op jit(solution)/shard_map/all_to_all | solution.py:145
  18.2 3.4 %all-to-all-start = ((bf16[8,2,4096]{2,1,0:T(2,128)(2,1)}), bf16[8,2,4096]{2,1,0:T(2,128)(2,1)S(1)}, u32[]{:S(2)}, u32[]{:S(2)}) async-start(bf16[8,2,4096]{2,1,0:T(2,128)(2,1)} %reshape.162), calls=%async_computation | async-start | bytes 262144 | tf_op jit(solution)/shard_map/all_to_all | solution.py:142
  21.6 2.8 %copy.64 = bf16[1,64,4096]{1,0,2:T(2,128)(2,1)S(1)} copy(bf16[1,64,4096]{2,1,0:T(8,128)(2,1)S(1)} %copy-done.1) | data formatting | bytes 1048576 | tf_op args[0]
  24.4 22.5 %reduce.6 = bf16[4096,64]{1,0:T(8,128)(2,1)S(1)} reduce(bf16[4096,1,64]{2,1,0:T(2,128)(2,1)S(1)} %bitcast.150, bf16[]{:T(256)} %broadcast.217), dimensions={1}, to_apply=%bitcast.128.reduce_sub_computation | reduce | bytes 1048578
  46.9 1.5 %reshape.166 = bf16[8,2,16384]{2,1,0:T(2,128)(2,1)} reshape(bf16[4096,64]{1,0:T(8,128)(2,1)S(1)} %reduce.6) | data formatting | bytes 1048576
  48.4 5.9 %all-to-all-start.3 = ((bf16[8,2,16384]{2,1,0:T(2,128)(2,1)}), bf16[8,2,16384]{2,1,0:T(2,128)(2,1)S(1)}, u32[]{:S(2)}, u32[]{:S(2)}) async-start(bf16[8,2,16384]{2,1,0:T(2,128)(2,1)} %reshape.166), calls=%async_computation.3 | async-start | bytes 1048576 | tf_op jit(solution)/shard_map/all_to_all | solution.py:141
  55.9 11.2 %all-to-all-done.3 = bf16[8,2,16384]{2,1,0:T(2,128)(2,1)S(1)} async-done(((bf16[8,2,16384]{2,1,0:T(2,128)(2,1)}), bf16[8,2,16384]{2,1,0:T(2,128)(2,1)S(1)}, u32[]{:S(2)}, u32[]{:S(2)}) %all-to-all-start.3) | async-done | bytes 524320 | tf_op jit(solution)/shard_map/all_to_all | solution.py:141
  67.1 0.9 tile.9
  68.1 3.9 %all-to-all-start.2 = ((bf16[4,512,128]{2,1,0:T(8,128)(2,1)}), bf16[4,512,128]{2,1,0:T(8,128)(2,1)S(1)}, u32[]{:S(2)}, u32[]{:S(2)}) async-start(bf16[4,512,128]{2,1,0:T(8,128)(2,1)} %tile.9), calls=%async_computation.2 | async-start | bytes 1048576 | tf_op jit(solution)/shard_map/all_to_all | solution.py:15
  72.0 10.9 %all_gather.3 = bf16[2048,128]{1,0:T(8,128)(2,1)S(1)} all-gather(bf16[512,128]{1,0:T(8,128)(2,1)S(1)} %bitcast.168), channel_id=1, replica_groups=mesh['ulysses'=8,'blk'=4] {'blk'}, dimensions={0}, use_global_device_ids=true | all-gather | bytes 655360 | tf_op jit(solution)/shard_map/all_gather | solution.py:157
  82.9 4.1 %reshape.167 = bf16[4096,1,64]{2,1,0:T(2,128)(2,1)S(1)} reshape(bf16[8,2,16384]{2,1,0:T(2,128)(2,1)} %copy-done) | data formatting | bytes 1048576
  87.0 3.6 %copy.65 = bf16[1,64,4096]{2,1,0:T(8,128)(2,1)} copy(bf16[1,64,4096]{1,0,2:T(2,128)(2,1)S(1)} %bitcast.149) | data formatting | bytes 1048576 | tf_op jit(solution)/shard_map/all_to_all | solution.py:141
  90.6 1.2 copy.79
  92.4 31.0 %while.23 = (s32[]{:T(128)}, f32[1,4,256]{2,1,0:T(4,128)S(1)}, f32[1,4,256]{2,1,0:T(4,128)S(1)}, f32[1,4,256,128]{3,2,1,0:T(8,128)S(1)}, f32[1,4,256]{2,1,0:T(4,...) while((s32[]{:T(128)}, f32[1,4,256]{2,1,0:T(4,128)S(1)}, ...), condition=%wide.region_13.14_spmd, body=%wide.region_1.13_spmd.sunk | while | flops 552381440 | bytes 17462768 | solution.py:109
  92.4 0.6 dynamic_slice.28
  93.8 1.1 fusion.59
  95.6 2.0 %conditional.5 = ((f32[1,4,256]{2,1,0:T(4,128)S(1)}, f32[1,4,256]{2,1,0:T(4,128)S(1)}, f32[1,4,256,128]{3,2,1,0:T(8,128)S(1)})) conditional(s32[]{:T(128)} %convert_element_type.47, (f32[1,4,256]{2,1,0:T(4,128)S(1)}, f32[1,4,256]{2,1,0:T(4,128)S(1)}, f32[1,4,256,128]{3,2,1,0:T(8,128)S(1)}) %tuple.82, (pred[256,512]{0,1:T(8,128)(4,1)S(1)}, ...), branch_computations={%region_9.9_spmd, %region_10.12_spmd} | conditional | flops 275516416 | bytes 8323104 | solution.py:96
  95.6 0.5 fusion.20
  96.1 0.5 fusion.22
  96.6 0.9 fusion.23
  98.2 2.0 %conditional.4 = ((f32[1,4,256]{2,1,0:T(4,128)S(1)}, f32[1,4,256]{2,1,0:T(4,128)S(1)}, f32[1,4,256,128]{3,2,1,0:T(8,128)S(1)})) conditional(s32[]{:T(128)} %convert_element_type.46, (f32[1,4,256]{2,1,0:T(4,128)S(1)}, f32[1,4,256]{2,1,0:T(4,128)S(1)}, f32[1,4,256,128]{3,2,1,0:T(8,128)S(1)}) %tuple.80, (pred[256,512]{0,1:T(8,128)(4,1)S(1)}, ...), branch_computations={%region_4.4_spmd, %region_5.7_spmd} | conditional | flops 275516416 | bytes 8323104 | solution.py:96
  98.2 0.5 fusion
  98.7 0.5 fusion.2
  99.3 0.9 fusion.3
  100.2 0.6 dynamic_slice.28
  101.6 1.1 fusion.59
  103.3 2.0 %conditional.5 = ((f32[1,4,256]{2,1,0:T(4,128)S(1)}, f32[1,4,256]{2,1,0:T(4,128)S(1)}, f32[1,4,256,128]{3,2,1,0:T(8,128)S(1)})) conditional(s32[]{:T(128)} %convert_element_type.47, (f32[1,4,256]{2,1,0:T(4,128)S(1)}, f32[1,4,256]{2,1,0:T(4,128)S(1)}, f32[1,4,256,128]{3,2,1,0:T(8,128)S(1)}) %tuple.82, (pred[256,512]{0,1:T(8,128)(4,1)S(1)}, ...), branch_computations={%region_9.9_spmd, %region_10.12_spmd} | conditional | flops 275516416 | bytes 8323104 | solution.py:96
  103.3 0.5 fusion.20
  103.8 0.5 fusion.22
  104.4 0.9 fusion.23
  106.0 1.9 %conditional.4 = ((f32[1,4,256]{2,1,0:T(4,128)S(1)}, f32[1,4,256]{2,1,0:T(4,128)S(1)}, f32[1,4,256,128]{3,2,1,0:T(8,128)S(1)})) conditional(s32[]{:T(128)} %convert_element_type.46, (f32[1,4,256]{2,1,0:T(4,128)S(1)}, f32[1,4,256]{2,1,0:T(4,128)S(1)}, f32[1,4,256,128]{3,2,1,0:T(8,128)S(1)}) %tuple.80, (pred[256,512]{0,1:T(8,128)(4,1)S(1)}, ...), branch_computations={%region_4.4_spmd, %region_5.7_spmd} | conditional | flops 275516416 | bytes 8323104 | solution.py:96
  106.5 0.5 fusion.2
  107.0 0.9 fusion.3
  108.0 0.6 dynamic_slice.28
  109.3 1.1 fusion.59
  111.1 1.9 %conditional.5 = ((f32[1,4,256]{2,1,0:T(4,128)S(1)}, f32[1,4,256]{2,1,0:T(4,128)S(1)}, f32[1,4,256,128]{3,2,1,0:T(8,128)S(1)})) conditional(s32[]{:T(128)} %convert_element_type.47, (f32[1,4,256]{2,1,0:T(4,128)S(1)}, f32[1,4,256]{2,1,0:T(4,128)S(1)}, f32[1,4,256,128]{3,2,1,0:T(8,128)S(1)}) %tuple.82, (pred[256,512]{0,1:T(8,128)(4,1)S(1)}, ...), branch_computations={%region_9.9_spmd, %region_10.12_spmd} | conditional | flops 275516416 | bytes 8323104 | solution.py:96
  111.6 0.5 fusion.22
  112.2 0.9 fusion.23
  113.7 2.0 %conditional.4 = ((f32[1,4,256]{2,1,0:T(4,128)S(1)}, f32[1,4,256]{2,1,0:T(4,128)S(1)}, f32[1,4,256,128]{3,2,1,0:T(8,128)S(1)})) conditional(s32[]{:T(128)} %convert_element_type.46, (f32[1,4,256]{2,1,0:T(4,128)S(1)}, f32[1,4,256]{2,1,0:T(4,128)S(1)}, f32[1,4,256,128]{3,2,1,0:T(8,128)S(1)}) %tuple.80, (pred[256,512]{0,1:T(8,128)(4,1)S(1)}, ...), branch_computations={%region_4.4_spmd, %region_5.7_spmd} | conditional | flops 275516416 | bytes 8323104 | solution.py:96
  113.7 0.5 fusion
  114.2 0.5 fusion.2
  114.8 0.9 fusion.3
  115.7 0.6 dynamic_slice.28
  117.1 1.1 fusion.59
  118.8 2.0 %conditional.5 = ((f32[1,4,256]{2,1,0:T(4,128)S(1)}, f32[1,4,256]{2,1,0:T(4,128)S(1)}, f32[1,4,256,128]{3,2,1,0:T(8,128)S(1)})) conditional(s32[]{:T(128)} %convert_element_type.47, (f32[1,4,256]{2,1,0:T(4,128)S(1)}, f32[1,4,256]{2,1,0:T(4,128)S(1)}, f32[1,4,256,128]{3,2,1,0:T(8,128)S(1)}) %tuple.82, (pred[256,512]{0,1:T(8,128)(4,1)S(1)}, ...), branch_computations={%region_9.9_spmd, %region_10.12_spmd} | conditional | flops 275516416 | bytes 8323104 | solution.py:96
  118.9 0.5 fusion.20
  119.4 0.5 fusion.22
  119.9 0.9 fusion.23
  121.5 2.0 %conditional.4 = ((f32[1,4,256]{2,1,0:T(4,128)S(1)}, f32[1,4,256]{2,1,0:T(4,128)S(1)}, f32[1,4,256,128]{3,2,1,0:T(8,128)S(1)})) conditional(s32[]{:T(128)} %convert_element_type.46, (f32[1,4,256]{2,1,0:T(4,128)S(1)}, f32[1,4,256]{2,1,0:T(4,128)S(1)}, f32[1,4,256,128]{3,2,1,0:T(8,128)S(1)}) %tuple.80, (pred[256,512]{0,1:T(8,128)(4,1)S(1)}, ...), branch_computations={%region_4.4_spmd, %region_5.7_spmd} | conditional | flops 275516416 | bytes 8323104 | solution.py:96
  121.5 0.5 fusion
  122.0 0.5 fusion.2
  122.6 0.9 fusion.3
  124.0 0.9 copy.71
  124.9 3.9 %reduce.7 = bf16[512,512]{1,0:T(8,128)(2,1)S(1)} reduce(bf16[512,1,512]{2,1,0:T(2,128)(2,1)S(1)} %bitcast.152, bf16[]{:T(256)} %broadcast.217), dimensions={1}, to_apply=%bitcast.130.reduce_sub_computation | reduce | bytes 1048578
  129.2 18.5 %all_to_all.69 = bf16[8,2,16384]{2,1,0:T(2,128)(2,1)S(1)} all-to-all(bf16[8,2,16384]{2,1,0:T(2,128)(2,1)S(1)} %reshape.168), channel_id=1, replica_groups=mesh['ulysses'=8,'blk'=4] {'ulysses'}, dimensions={0} | all-to-all | bytes 1048576 | tf_op jit(solution)/shard_map/all_to_all | solution.py:162
  147.6 0.5 reshape.169
  148.3 0.8 copy.76
  (88 shorter events, 5.2 us)
Async XLA Ops:
  0.0 10.9 %copy-start.2 = (bf16[1,64,1024]{2,1,0:T(8,128)(2,1)S(1)}, bf16[1,64,1024]{2,1,0:T(8,128)(2,1)}, u32[]{:S(2)}) copy-start(bf16[1,64,1024]{2,1,0:T(8,128)(2,1)} %param.11) | copy-start | bytes 393220
  0.0 21.6 %copy-start.1 = (bf16[1,64,4096]{2,1,0:T(8,128)(2,1)S(1)}, bf16[1,64,4096]{2,1,0:T(8,128)(2,1)}, u32[]{:S(2)}) copy-start(bf16[1,64,4096]{2,1,0:T(8,128)(2,1)} %param.10) | copy-start | bytes 1572868
  5.1 13.1 %all-to-all-start.1 = ((bf16[8,2,4096]{2,1,0:T(2,128)(2,1)}), bf16[8,2,4096]{2,1,0:T(2,128)(2,1)S(1)}, u32[]{:S(2)}, u32[]{:S(2)}) async-start(bf16[8,2,4096]{2,1,0:T(2,128)(2,1)} %reshape.164), calls=%async_computation.1 | async-start | bytes 262144 | tf_op jit(solution)/shard_map/all_to_all | solution.py:145
  18.2 30.2 %all-to-all-start = ((bf16[8,2,4096]{2,1,0:T(2,128)(2,1)}), bf16[8,2,4096]{2,1,0:T(2,128)(2,1)S(1)}, u32[]{:S(2)}, u32[]{:S(2)}) async-start(bf16[8,2,4096]{2,1,0:T(2,128)(2,1)} %reshape.162), calls=%async_computation | async-start | bytes 262144 | tf_op jit(solution)/shard_map/all_to_all | solution.py:142
  46.9 7.4 %copy-start.3 = (s32[16]{0:T(128)S(1)}, s32[16]{0:T(128)}, u32[]{:S(2)}) copy-start(s32[16]{0:T(128)} %param.13) | copy-start | bytes 196
  48.4 18.7 %all-to-all-start.3 = ((bf16[8,2,16384]{2,1,0:T(2,128)(2,1)}), bf16[8,2,16384]{2,1,0:T(2,128)(2,1)S(1)}, u32[]{:S(2)}, u32[]{:S(2)}) async-start(bf16[8,2,16384]{2,1,0:T(2,128)(2,1)} %reshape.166), calls=%async_computation.3 | async-start | bytes 1048576 | tf_op jit(solution)/shard_map/all_to_all | solution.py:141
  67.1 1.0 copy-start
  68.1 24.2 %all-to-all-start.2 = ((bf16[4,512,128]{2,1,0:T(8,128)(2,1)}), bf16[4,512,128]{2,1,0:T(8,128)(2,1)S(1)}, u32[]{:S(2)}, u32[]{:S(2)}) async-start(bf16[4,512,128]{2,1,0:T(8,128)(2,1)} %tile.9), calls=%async_computation.2 | async-start | bytes 1048576 | tf_op jit(solution)/shard_map/all_to_all | solution.py:15
